TPU v7x, 32 devices: a whole 2x2x4 slice. The times are simulated.
32 devices in a mesh: ctx: 16 (over z, x, core), fsdp: 2 (over y).
Axes of the slice: x: 2, y: 2, z: 4, core: 2. Of those that a mesh axis runs over, the one named last changes fastest.
Arguments:
- tokens: bfloat16 [2, 2048, 1024], P('fsdp', 'ctx'), may hold values from -6 to 6
- cotangent: bfloat16 [2, 2048, 1024], P('fsdp', 'ctx'), may hold values from -6 to 6
- gain_attn: float32 [1024], replicated, may hold values from 0.5 to 1.5
- gain_mlp: float32 [1024], replicated, may hold values from 0.5 to 1.5
- qkv_weight: bfloat16 [3072, 1024], P('fsdp'), may hold values from -2 to 2
- out_weight: bfloat16 [1024, 1024], P('fsdp'), may hold values from -0.625 to 0.625
- in_weight: bfloat16 [5248, 1024], P('fsdp'), may hold values from -0.1875 to 0.1875
- down_weight: bfloat16 [1024, 2624], P('fsdp'), may hold values from -0.125 to 0.125
Outputs:
- output: float32 [2, 2048, 1024], P('fsdp', 'ctx')
- grad_input: float32 [2, 2048, 1024], P('fsdp', 'ctx')
- grad_qkv: float32 [3072, 1024], P(('ctx', 'fsdp'))
- grad_out_proj: float32 [1024, 1024], P(('ctx', 'fsdp'))
- grad_in_proj: float32 [5248, 1024], P(('ctx', 'fsdp'))
- grad_down: float32 [1024, 2624], P(('ctx', 'fsdp'))
- grad_gain_attn: float32 [1024], P(('ctx', 'fsdp'))
- grad_gain_mlp: float32 [1024], P(('ctx', 'fsdp'))
All inputs are finite; a program needn't handle non-finite values.
Results may differ from a plain program's by a relative error of at most 0.015.
Values may be sent and summed in bfloat16 or wider, within the bound.
A program may use at most 256 MiB of HBM per device.

v0:
```python
import math
import jax
import jax.numpy as jnp
from jax import lax
from jax.sharding import PartitionSpec as P

HEAD_DIM = 64
EPSILON = 1e-05
ROPE_BASE = 160000.0


def normalize(tensor):
    centred = tensor - jnp.mean(tensor, axis=-1, keepdims=True)
    inv_std = lax.rsqrt(jnp.mean(centred * centred, axis=-1, keepdims=True) + EPSILON)
    return (centred * inv_std, inv_std)


def norm_back(grad_norm, normed, inv_std):
    return inv_std * (
        grad_norm
        - jnp.mean(grad_norm, axis=-1, keepdims=True)
        - normed * jnp.mean(grad_norm * normed, axis=-1, keepdims=True)
    )


def gelu_pair(tensor):
    cumul = 0.5 * (1.0 + jax.scipy.special.erf(tensor * 0.7071067811865476))
    density = jnp.exp(-0.5 * tensor * tensor) * 0.3989422804014327
    return (tensor * cumul, cumul + tensor * density)


def rope_tables(offset, length, head_size):
    positions = (offset + jnp.arange(length, dtype=jnp.int32)).astype(jnp.float32)
    inverse = ROPE_BASE ** (
        -jnp.arange(0, head_size, 2, dtype=jnp.int32).astype(jnp.float32) / head_size
    )
    angles = positions[:, None] * inverse[None, :]
    angles = jnp.concatenate([angles, angles], axis=-1)
    return (jnp.cos(angles)[:, None, :], jnp.sin(angles)[:, None, :])


def rotate(tensor, cos_table, sine_table):
    middle = tensor.shape[-1] // 2
    turned = jnp.concatenate([-tensor[..., middle:], tensor[..., :middle]], axis=-1)
    return tensor * cos_table + turned * sine_table


def rotate_back(gradient, cos_table, sine_table):
    middle = gradient.shape[-1] // 2
    scaled = gradient * sine_table
    turned = jnp.concatenate([scaled[..., middle:], -scaled[..., :middle]], axis=-1)
    return gradient * cos_table + turned


def rows_product(left, right):
    return lax.dot_general(
        left, right, (((1,), (1,)), ((), ())), preferred_element_type=jnp.float32
    )


def rows_contract(left, right):
    return lax.dot_general(
        left, right, (((0,), (0,)), ((), ())), preferred_element_type=jnp.float32
    )


def per_device(
    tokens, cotangent, gain_attn, gain_mlp, qkv_weight, out_weight, in_weight, down_weight
):
    f32 = jnp.float32
    bf16 = jnp.bfloat16
    qkv_full, out_full, in_full, down_full = (
        lax.all_gather(qkv_weight, "fsdp", axis=0, tiled=True),
        lax.all_gather(out_weight, "fsdp", axis=0, tiled=True),
        lax.all_gather(in_weight, "fsdp", axis=0, tiled=True),
        lax.all_gather(down_weight, "fsdp", axis=0, tiled=True),
    )
    tok_rows = tokens.shape[1]
    width = tokens.shape[2]
    hidden = down_full.shape[1]
    head_size = HEAD_DIM
    head_count = width // head_size
    scale = head_size ** (-0.5)
    offset = lax.axis_index("ctx") * tok_rows
    cos_table, sine_table = rope_tables(offset, tok_rows, head_size)
    resid = tokens[0].astype(f32)
    normed_a, inv_a = normalize(resid)
    act_a = (normed_a * gain_attn).astype(bf16)
    packed = rows_product(act_a, qkv_full)
    query_heads = rotate(
        packed[:, :width].reshape(tok_rows, head_count, head_size), cos_table, sine_table
    ).astype(bf16)
    key_heads = rotate(
        packed[:, width : 2 * width].reshape(tok_rows, head_count, head_size), cos_table, sine_table
    ).astype(bf16)
    value_send = packed[:, 2 * width :].astype(bf16)
    key_send = key_heads.reshape(tok_rows, width)
    value_heads = value_send.reshape(tok_rows, head_count, head_size)
    start_state = (
        jnp.zeros((tok_rows, head_count, head_size), f32),
        jnp.full((head_count, tok_rows), -1e30, f32),
        jnp.zeros((head_count, tok_rows), f32),
    )
    key_piece = lax.all_gather(key_send, "ctx", axis=0, tiled=True)
    value_piece = lax.all_gather(value_send, "ctx", axis=0, tiled=True)
    length = key_piece.shape[0]
    step_len = math.gcd(length, 1024)

    def attend_block(block_num, running):
        weighted, row_max, row_sum = running
        key_blk = lax.dynamic_slice_in_dim(key_piece, block_num * step_len, step_len, 0).reshape(
            step_len, head_count, head_size
        )
        value_blk = lax.dynamic_slice_in_dim(
            value_piece, block_num * step_len, step_len, 0
        ).reshape(step_len, head_count, head_size)
        scores = (
            jnp.einsum("qhd,khd->hqk", query_heads, key_blk, preferred_element_type=f32) * scale
        )
        new_max = jnp.maximum(row_max, jnp.max(scores, axis=-1))
        shrink = jnp.exp(row_max - new_max)
        weights = jnp.exp(scores - new_max[..., None])
        row_sum = row_sum * shrink + jnp.sum(weights, axis=-1)
        weighted = weighted * shrink.T[:, :, None] + jnp.einsum(
            "hqk,khd->qhd", weights.astype(bf16), value_blk, preferred_element_type=f32
        )
        return (weighted, new_max, row_sum)

    weighted, row_max, row_sum = lax.fori_loop(0, length // step_len, attend_block, start_state)
    log_sum = row_max + jnp.log(row_sum)
    mixed = (weighted / row_sum.T[:, :, None]).reshape(tok_rows, width).astype(bf16)
    middle = resid + rows_product(mixed, out_full)
    normed_m, inv_m = normalize(middle)
    act_m = (normed_m * gain_mlp).astype(bf16)
    inner = rows_product(act_m, in_full)
    gelu_val, gelu_slope = gelu_pair(inner[:, :hidden])
    gated = (gelu_val * inner[:, hidden:]).astype(bf16)
    output = middle + rows_product(gated, down_full)
    cot_rows = cotangent[0]
    grad_down = rows_contract(cot_rows, gated)
    grad_gated = jnp.dot(cot_rows, down_full, preferred_element_type=f32)
    grad_inner = jnp.concatenate(
        [grad_gated * inner[:, hidden:] * gelu_slope, grad_gated * gelu_val], axis=1
    ).astype(bf16)
    grad_in = rows_contract(grad_inner, act_m)
    grad_act_m = jnp.dot(grad_inner, in_full, preferred_element_type=f32)
    grad_gain_m = jnp.sum(grad_act_m * normed_m, axis=0)
    grad_middle = cot_rows.astype(f32) + norm_back(grad_act_m * gain_mlp, normed_m, inv_m)
    grad_mid_bf = grad_middle.astype(bf16)
    grad_out = rows_contract(grad_mid_bf, mixed)
    grad_mixed = jnp.dot(grad_mid_bf, out_full, preferred_element_type=f32).astype(bf16)
    grad_heads = grad_mixed.reshape(tok_rows, head_count, head_size)
    delta_rows = jnp.sum(
        grad_heads.astype(f32) * mixed.reshape(tok_rows, head_count, head_size).astype(f32), axis=-1
    )
    delta = delta_rows.T
    zeros_heads = jnp.zeros((tok_rows, head_count, head_size), f32)
    query_key_piece = lax.all_gather(key_send, "ctx", axis=0, tiled=True)
    query_value_piece = lax.all_gather(value_send, "ctx", axis=0, tiled=True)
    length = query_key_piece.shape[0]
    query_step_len = math.gcd(length, 1024)

    def query_grad_block(block_num, grad_query):
        key_blk = lax.dynamic_slice_in_dim(
            query_key_piece, block_num * query_step_len, query_step_len, 0
        ).reshape(query_step_len, head_count, head_size)
        value_blk = lax.dynamic_slice_in_dim(
            query_value_piece, block_num * query_step_len, query_step_len, 0
        ).reshape(query_step_len, head_count, head_size)
        scores = (
            jnp.einsum("qhd,khd->hqk", query_heads, key_blk, preferred_element_type=f32) * scale
        )
        probs = jnp.exp(scores - log_sum[..., None])
        grad_probs = jnp.einsum("qhd,khd->hqk", grad_heads, value_blk, preferred_element_type=f32)
        grad_scores = (probs * (grad_probs - delta[..., None])).astype(bf16)
        return (
            grad_query
            + jnp.einsum("hqk,khd->qhd", grad_scores, key_blk, preferred_element_type=f32) * scale
        )

    grad_query = lax.fori_loop(0, length // query_step_len, query_grad_block, zeros_heads)
    query_send = query_heads.reshape(tok_rows, width).astype(f32)
    grad_send = grad_mixed.astype(f32)
    query_piece = lax.all_gather(query_send, "ctx", axis=0, tiled=True)
    grad_piece = lax.all_gather(grad_send, "ctx", axis=0, tiled=True)
    log_piece = lax.all_gather(log_sum.T, "ctx", axis=0, tiled=True)
    delta_piece = lax.all_gather(delta_rows, "ctx", axis=0, tiled=True)
    length = query_piece.shape[0]
    key_step_len = math.gcd(length, 1024)

    def key_grad_block(block_num, running):
        grad_keys, grad_values = running
        query_blk = (
            lax.dynamic_slice_in_dim(query_piece, block_num * key_step_len, key_step_len, 0)
            .astype(bf16)
            .reshape(key_step_len, head_count, head_size)
        )
        grad_blk = (
            lax.dynamic_slice_in_dim(grad_piece, block_num * key_step_len, key_step_len, 0)
            .astype(bf16)
            .reshape(key_step_len, head_count, head_size)
        )
        log_blk = lax.dynamic_slice_in_dim(log_piece, block_num * key_step_len, key_step_len, 0).T
        delta_blk = lax.dynamic_slice_in_dim(
            delta_piece, block_num * key_step_len, key_step_len, 0
        ).T
        scores = (
            jnp.einsum("qhd,khd->hqk", query_blk, key_heads, preferred_element_type=f32) * scale
        )
        probs = jnp.exp(scores - log_blk[..., None])
        grad_values = grad_values + jnp.einsum(
            "hqk,qhd->khd", probs.astype(bf16), grad_blk, preferred_element_type=f32
        )
        grad_probs = jnp.einsum("qhd,khd->hqk", grad_blk, value_heads, preferred_element_type=f32)
        grad_scores = (probs * (grad_probs - delta_blk[..., None])).astype(bf16)
        grad_keys = (
            grad_keys
            + jnp.einsum("hqk,qhd->khd", grad_scores, query_blk, preferred_element_type=f32) * scale
        )
        return (grad_keys, grad_values)

    grad_keys, grad_values = lax.fori_loop(
        0, length // key_step_len, key_grad_block, (zeros_heads, zeros_heads)
    )
    grad_query = rotate_back(grad_query, cos_table, sine_table)
    grad_keys = rotate_back(grad_keys, cos_table, sine_table)
    grad_packed = jnp.concatenate(
        [
            grad_query.reshape(tok_rows, width),
            grad_keys.reshape(tok_rows, width),
            grad_values.reshape(tok_rows, width),
        ],
        axis=1,
    ).astype(bf16)
    grad_qkv = rows_contract(grad_packed, act_a)
    grad_act_a = jnp.dot(grad_packed, qkv_full, preferred_element_type=f32)
    grad_gain_a = jnp.sum(grad_act_a * normed_a, axis=0)
    grad_input = grad_middle + norm_back(grad_act_a * gain_attn, normed_a, inv_a)
    owned = (
        lax.psum_scatter(grad_qkv, ("ctx", "fsdp"), scatter_dimension=0, tiled=True),
        lax.psum_scatter(grad_out, ("ctx", "fsdp"), scatter_dimension=0, tiled=True),
        lax.psum_scatter(grad_in, ("ctx", "fsdp"), scatter_dimension=0, tiled=True),
        lax.psum_scatter(grad_down, ("ctx", "fsdp"), scatter_dimension=0, tiled=True),
        lax.psum_scatter(grad_gain_a, ("ctx", "fsdp"), scatter_dimension=0, tiled=True),
        lax.psum_scatter(grad_gain_m, ("ctx", "fsdp"), scatter_dimension=0, tiled=True),
    )
    return (
        output[None],
        grad_input[None],
        owned[0],
        owned[1],
        owned[2],
        owned[3],
        owned[4],
        owned[5],
    )


def solution(mesh):
    return jax.shard_map(
        per_device,
        mesh=mesh,
        in_specs=(
            P("fsdp", "ctx", None),
            P("fsdp", "ctx", None),
            P(),
            P(),
            P("fsdp", None),
            P("fsdp", None),
            P("fsdp", None),
            P("fsdp", None),
        ),
        out_specs=(
            P("fsdp", "ctx", None),
            P("fsdp", "ctx", None),
            P(("ctx", "fsdp"), None),
            P(("ctx", "fsdp"), None),
            P(("ctx", "fsdp"), None),
            P(("ctx", "fsdp"), None),
            P(("ctx", "fsdp")),
            P(("ctx", "fsdp")),
        ),
        check_vma=False,
    )
```

profile of v0, /device:TPU:14, one launch (start us, length us, event | category | flops | bytes accessed | tf_op | source)
XLA Modules:
  0.0 1275.8 jit_solution(7228493947482920155)
XLA Ops:
  9.6 80.5 %all-gather.9.cloned.1.call-done = bf16[3072,1024]{1,0:T(8,128)(2,1)} async-done(((bf16[1536,1024]{1,0:T(8,128)(2,1)}), bf16[3072,1024]{1,0:T(8,128)(2,1)}) %all-gather.9.cloned.1.call-update) | async-done | bytes 6291472 | tf_op jit(solution)/shard_map/all_gather | solution.py:73
  90.1 5.0 fusion.85
  96.2 1.2 copy.60
  97.6 1.1 add_convert_fusion.2
  98.7 1.2 copy.71
  100.0 1.2 copy.61
  101.2 2.1 fusion.71
  106.7 47.2 %all-gather.11.cloned.1.call-done = bf16[2048,1024]{1,0:T(8,128)(2,1)} async-done(((bf16[128,1024]{1,0:T(8,128)(2,1)}), bf16[2048,1024]{1,0:T(8,128)(2,1)}) %all-gather.11.cloned.1.call-update) | async-done | bytes 4194320 | tf_op jit(solution)/shard_map/all_gather | solution.py:104
  153.9 6.5 copy.63
  160.4 44.6 %all-gather.13.cloned.1.call-done = bf16[2048,1024]{1,0:T(8,128)(2,1)} async-done(((bf16[128,1024]{1,0:T(8,128)(2,1)}), bf16[2048,1024]{1,0:T(8,128)(2,1)}) %all-gather.13.cloned.1.call-update) | async-done | bytes 4194320 | tf_op jit(solution)/shard_map/all_gather | solution.py:105
  205.0 6.5 copy.64
  211.5 29.9 %while.48 = (s32[]{:T(128)}, f32[128,16,64]{0,2,1:T(8,128)S(1)}, f32[16,128]{1,0:T(8,128)S(1)}, f32[16,128]{1,0:T(8,128)S(1)}, bf16[2048,1024]{0,1:T(8,128)(2,1)...) while((s32[]{:T(128)}, f32[128,16,64]{0,2,1:T(8,128)S(1)}, ...), condition=%wide.region_5.0_spmd.clone, body=%wide.region_2.0_spmd.clone.sunk | while | flops 554053632 | bytes 72745168 | solution.py:129
  211.5 3.1 constant_dynamic-slice_fusion.10
  214.6 4.8 bitcast_reduce_fusion.2
  219.4 5.3 fusion.148
  225.2 1.4 fusion.149
  226.6 2.7 constant_dynamic-slice_fusion.10
  229.3 4.8 bitcast_reduce_fusion.2
  234.1 5.3 fusion.148
  239.9 1.4 fusion.149
  241.5 2.5 fusion.91
  244.3 127.5 %all-gather.17.cloned.1.call-done = bf16[5248,1024]{1,0:T(8,128)(2,1)} async-done(((bf16[2624,1024]{1,0:T(8,128)(2,1)}), bf16[5248,1024]{1,0:T(8,128)(2,1)}) %all-gather.17.cloned.1.call-update) | async-done | bytes 10747920 | tf_op jit(solution)/shard_map/all_gather | solution.py:75
  371.8 9.3 fusion.87
  381.1 62.2 %all-gather.19.cloned.1.call-done = bf16[1024,2624]{0,1:T(8,128)(2,1)} async-done(((bf16[512,2624]{0,1:T(8,128)(2,1)}), bf16[1024,2624]{0,1:T(8,128)(2,1)}) %all-gather.19.cloned.1.call-update) | async-done | bytes 5373968 | tf_op jit(solution)/shard_map/all_gather | solution.py:76
  443.3 5.3 fusion.48
  448.6 7.1 multiply_reduce_fusion
  456.0 1.1 convolution_convert_fusion
  457.2 2.7 fusion.75
  460.0 7.7 convolution_bitcast_fusion
  467.7 12.1 copy.78
  483.0 15.4 %all_gather.39 = f32[2048,16]{0,1:T(8,128)S(1)} all-gather(f32[128,16]{0,1:T(8,128)S(1)} %bitcast.218), channel_id=1, replica_groups=mesh['ctx'=16,'fsdp'=2] {'ctx'}, dimensions={0}, use_global_device_ids=true | all-gather | bytes 139264 | tf_op jit(solution)/shard_map/all_gather | solution.py:186
  498.4 1.0 multiply_reduce_fusion.1
  499.5 22.1 %all_gather.41 = f32[2048,16]{0,1:T(8,128)S(1)} all-gather(f32[128,16]{0,1:T(8,128)S(1)} %multiply_reduce_fusion.1), channel_id=1, replica_groups=mesh['ctx'=16,'fsdp'=2] {'ctx'}, dimensions={0}, use_global_device_ids=true | all-gather | bytes 139264 | tf_op jit(solution)/shard_map/all_gather | solution.py:187
  521.6 33.4 %while.49 = (s32[]{:T(128)}, f32[128,16,64]{0,2,1:T(8,128)}, bf16[2048,1024]{0,1:T(8,128)(2,1)}, bf16[128,16,64]{0,2,1:T(8,128)(2,1)S(1)}, f32[16,128]{1,0:T(8,1...) while((s32[]{:T(128)}, f32[128,16,64]{0,2,1:T(8,128)}, ...), condition=%wide.region_12.0_spmd.clone, body=%wide.region_11.0_spmd.clone.sunk | while | flops 816185344 | bytes 33079508 | solution.py:181
  521.6 4.0 constant_dynamic-slice_fusion.11
  525.6 4.6 fusion.156
  530.2 8.1 fusion.157
  538.3 4.0 constant_dynamic-slice_fusion.11
  542.3 4.6 fusion.156
  546.9 8.0 fusion.157
  555.0 65.2 %while.50 = (s32[]{:T(128)}, f32[128,16,64]{0,2,1:T(8,128)}, f32[128,16,64]{0,2,1:T(8,128)S(1)}, bf16[2048,1024]{1,0:T(8,128)(2,1)}, bf16[128,16,64]{0,2,1:T(8,1...) while((s32[]{:T(128)}, f32[128,16,64]{0,2,1:T(8,128)}, ...), condition=%wide.region_14.0_spmd.clone, body=%wide.region_13.0_spmd.clone.sunk | while | flops 1091174400 | bytes 53412036 | solution.py:222
  555.2 4.7 constant_dynamic-slice_fusion.12
  559.9 2.9 copy.84
  562.8 4.6 fusion.165
  567.5 4.0 copy.85
  571.4 10.8 fusion.166
  582.2 5.5 fusion.167
  587.7 4.7 constant_dynamic-slice_fusion.12
  592.4 2.9 copy.84
  595.2 4.6 fusion.165
  599.9 4.0 copy.85
  603.9 10.8 fusion.166
  614.7 5.5 fusion.167
  620.3 1.5 broadcast_multiply_fusion.1
  622.9 6.4 fusion.69
  630.8 9.2 fusion.50
  640.0 547.2 %fusion = f32[168,1024]{1,0:T(8,128)} fusion(f32[5248,1024]{1,0:T(8,128)} %fusion.50), kind=kCustom, calls=%all-reduce-scatter | all-reduce-scatter fusion | flops 5505025 | bytes 22183936
  1187.3 1.9 slice.67
  1189.1 3.8 collective-permute-start
  1193.0 4.5 fusion.49
  1197.4 8.4 collective-permute-done
  1205.8 3.1 concatenate.38
  1209.9 4.0 fusion.65
  1213.9 52.7 %all-reduce.4 = (f32[1024]{0:T(1024)S(1)}, f32[1024]{0:T(1024)S(1)}) all-reduce(f32[1024]{0:T(1024)S(1)} %get-tuple-element.613, f32[1024]{0:T(1024)S(1)} %copy-done.43), channel_id=6, replica_groups=mesh['ctx'=16,'fsdp'=2] {'ctx','fsdp'}, use_global_device_ids=true, to_apply=%region_22.0.clone | all-reduce | flops 2048 | bytes 16384
  (168 shorter events, 17.5 us)
Async XLA Ops:
  7.2 2.1 copy-start.4
  7.2 82.9 %copy-start.29 = (f32[1024]{0:T(1024)S(1)}, f32[1024]{0:T(1024)}, u32[]{:S(2)}) copy-start(f32[1024]{0:T(1024)} %param.16) | copy-start | bytes 12292
  7.2 82.9 %all-gather.9.cloned.1.call-start = ((), (), s32[]{:S(2)}) async-start(), calls=%async_computation.3 | async-start | bytes 9437184 | tf_op jit(solution)/shard_map/all_gather | solution.py:73
  7.9 146.0 %all-gather.11.cloned.1.call-start = ((), (), s32[]{:S(2)}) async-start(), calls=%async_computation.4 | async-start | bytes 4456448 | tf_op jit(solution)/shard_map/all_gather | solution.py:104
  8.2 89.4 %copy-start.25 = (f32[128,64]{0,1:T(8,128)}, f32[128,64]{0,1:T(8,128)S(1)}, u32[]{:S(2)}) copy-start(f32[128,64]{0,1:T(8,128)S(1)} %get-tuple-element.704) | copy-start | bytes 98308
  8.2 89.4 %copy-start.27 = (f32[128,64]{0,1:T(8,128)}, f32[128,64]{0,1:T(8,128)S(1)}, u32[]{:S(2)}) copy-start(f32[128,64]{0,1:T(8,128)S(1)} %get-tuple-element.703) | copy-start | bytes 98308
  9.3 85.8 %copy-start.35 = (f32[128]{0:T(128)}, f32[128]{0:T(128)S(1)}, u32[]{:S(2)}) copy-start(f32[128]{0:T(128)S(1)} %broadcast_multiply_fusion.8) | copy-start | bytes 1540
  9.6 85.5 %copy-start.37 = (f32[128]{0:T(128)}, f32[128]{0:T(128)S(1)}, u32[]{:S(2)}) copy-start(f32[128]{0:T(128)S(1)} %add_rsqrt_fusion.1) | copy-start | bytes 1540
  103.3 101.7 %all-gather.13.cloned.1.call-start = ((), (), s32[]{:S(2)}) async-start(), calls=%async_computation.5 | async-start | bytes 4456448 | tf_op jit(solution)/shard_map/all_gather | solution.py:105
  104.1 137.4 %all-gather.15.cloned.1.call-start = ((), (), s32[]{:S(2)}) async-start(), calls=%async_computation.6 | async-start | bytes 3145728 | tf_op jit(solution)/shard_map/all_gather | solution.py:74
  104.7 267.1 %all-gather.17.cloned.1.call-start = ((), (), s32[]{:S(2)}) async-start(), calls=%async_computation.7 | async-start | bytes 16121856 | tf_op jit(solution)/shard_map/all_gather | solution.py:75
  105.3 338.0 %all-gather.19.cloned.1.call-start = ((), (), s32[]{:S(2)}) async-start(), calls=%async_computation.8 | async-start | bytes 8060928 | tf_op jit(solution)/shard_map/all_gather | solution.py:76
  105.9 449.1 %all-gather.21.cloned.1.call-start = ((), (), s32[]{:S(2)}) async-start(), calls=%async_computation.9 | async-start | bytes 4456448 | tf_op jit(solution)/shard_map/all_gather | solution.py:184
  106.6 448.3 %all-gather.23.cloned.1.call-start = ((), (), s32[]{:S(2)}) async-start(), calls=%async_computation.10 | async-start | bytes 4456448 | tf_op jit(solution)/shard_map/all_gather | solution.py:185
  219.4 5.8 copy-start
  234.1 5.8 copy-start
  241.4 130.4 %copy-start.31 = (f32[1024]{0:T(1024)S(1)}, f32[1024]{0:T(1024)}, u32[]{:S(2)}) copy-start(f32[1024]{0:T(1024)} %param.17) | copy-start | bytes 12292
  244.0 211.6 %copy-start.1 = (f32[128,1024]{1,0:T(8,128)}, f32[128,1024]{1,0:T(8,128)S(1)}, u32[]{:S(2)}) copy-start(f32[128,1024]{1,0:T(8,128)S(1)} %get-tuple-element.706) | copy-start | bytes 1572868
  244.1 211.6 %copy-start.39 = (f32[128]{0:T(128)}, f32[128]{0:T(128)S(1)}, u32[]{:S(2)}) copy-start(f32[128]{0:T(128)S(1)} %broadcast_multiply_fusion.7) | copy-start | bytes 1540
  244.3 211.4 %copy-start.41 = (f32[128]{0:T(128)}, f32[128]{0:T(128)S(1)}, u32[]{:S(2)}) copy-start(f32[128]{0:T(128)S(1)} %add_rsqrt_fusion) | copy-start | bytes 1540
  244.3 199.0 %copy-start.20 = (bf16[1,128,1024]{2,1,0:T(8,128)(2,1)S(1)}, bf16[1,128,1024]{2,1,0:T(8,128)(2,1)}, u32[]{:S(2)}) copy-start(bf16[1,128,1024]{2,1,0:T(8,128)(2,1)} %param.15) | copy-start | bytes 786436
  448.5 7.1 copy-start.21
  448.6 7.1 copy-start.23
  448.6 7.4 copy-start.7
  456.0 4.0 copy-start.8
  457.1 811.7 %reduce-scatter.10.cloned.1.call-start = ((), (), s32[]{:S(2)}) async-start(), calls=%async_computation.12 | async-start | bytes 4325376 | tf_op jit(solution)/shard_map/reduce_scatter | solution.py:241
  460.0 808.9 %reduce-scatter.12.cloned.1.call-start = ((), (), s32[]{:S(2)}) async-start(), calls=%async_computation.13 | async-start | bytes 11354112
  479.8 0.9 copy-start.16
  479.8 1.8 copy-start.17
  479.8 789.0 %reduce-scatter.8.cloned.1.call-start = ((), (), s32[]{:S(2)}) async-start(), calls=%async_computation.11 | async-start | bytes 12976128 | tf_op jit(solution)/shard_map/reduce_scatter | solution.py:240
  482.4 0.6 copy-start.33
  521.6 33.4 %copy-start.6 = (bf16[128,16,64]{0,2,1:T(8,128)(2,1)S(1)}, bf16[128,16,64]{0,2,1:T(8,128)(2,1)}, u32[]{:S(2)}) copy-start(bf16[128,16,64]{0,2,1:T(8,128)(2,1)} %get-tuple-element.919) | copy-start | bytes 786436
  525.6 4.7 copy-start.34
  542.3 4.7 copy-start.34
  555.0 65.3 %copy-start.28 = (f32[128,64]{0,1:T(8,128)S(1)}, f32[128,64]{0,1:T(8,128)}, u32[]{:S(2)}) copy-start(f32[128,64]{0,1:T(8,128)} %copy-done.27) | copy-start | bytes 98308
  620.2 1.7 copy-start.18
  620.2 1.7 copy-start.19
  620.2 1.7 copy-start.26
  620.2 1.9 copy-start.10
  621.7 1.2 copy-start.5
  621.7 1.2 copy-start.30
  621.8 1.2 copy-start.36
  621.8 1.2 copy-start.38
  622.1 0.7 copy-start.12
  622.1 0.8 copy-start.14
  629.3 1.0 copy-start.2
  629.3 1.3 copy-start.22
  629.3 1.5 copy-start.24
  629.3 1.5 copy-start.32
  629.3 1.5 copy-start.40
  629.3 1.5 copy-start.42
  640.0 552.9 %copy-start.3 = (f32[128,5248]{1,0:T(8,128)S(1)}, f32[128,5248]{1,0:T(8,128)}, u32[]{:S(2)}) copy-start(f32[128,5248]{1,0:T(8,128)} %fusion.87) | copy-start | bytes 8060932
  1189.1 16.7 %collective-permute-start = (f32[124,1024]{1,0:T(8,128)}, f32[124,1024]{1,0:T(8,128)}, u32[]{:S(2)}, u32[]{:S(2)}) collective-permute-start(f32[124,1024]{1,0:T(8,128)} %slice.67), channel_id=1, source_target_pairs={{0,1},{1,2},{2,3},{3,4},{4,5},{5,6},{6,7},{7,8},{8,9},{9,10},{10,1... | collective-permute-start | bytes 1523720
  1197.4 12.5 copy-start.11
  1197.4 12.5 copy-start.13
  1197.4 12.5 copy-start.15
  1209.9 4.0 copy-start.43
  1209.9 57.9 %copy-start.9 = (f32[128,1024]{1,0:T(8,128)S(1)}, f32[128,1024]{1,0:T(8,128)}, u32[]{:S(2)}) copy-start(f32[128,1024]{1,0:T(8,128)} %copy-done.8) | copy-start | bytes 1572868
Sparse Core Ops, SparseCore 0:
  9.5 80.5 all-gather.8
  103.4 50.4 all-gather.10
  156.1 48.8 all-gather.12
  206.4 31.5 all-gather.14
  239.4 132.3 all-gather.16
  373.2 70.0 all-gather.18
  445.4 50.5 all-gather.20
  498.1 49.5 all-gather.22
  550.6 139.3 reduce-scatter.9
  696.4 204.9 reduce-scatter.11
  908.0 196.3 reduce-scatter.7
where the time goes:
time: 1280 us
  blocking collectives  637 us (50%)
  waiting for transfers between devices  373 us (29%)
  matrix products  152 us (12%)
  local copies, waits for them, and re-layouts  82 us (6%)
  between operations  15 us (1%)
    unnamed x2, blocking collectives  600 us
    all_gather x1, waiting for transfers between devices, per_device(): lax.all_gather(in_weight, 'fsdp', axis=0, tiled=True)  128 us
    all_gather x1, waiting for transfers between devices, per_device(): lax.all_gather(qkv_weight, 'fsdp', axis=0, tiled=True)  80.5 us
    all_gather x1, waiting for transfers between devices, per_device(): lax.all_gather(down_weight, 'fsdp', axis=0, tiled=True)  62.2 us
    all_gather x1, waiting for transfers between devices, per_device(): key_piece = lax.all_gather(key_send, 'ctx', axis=0, tiled=True)  47.2 us
    all_gather x1, waiting for transfers between devices, per_device(): value_piece = lax.all_gather(value_send, 'ctx', axis=0, tiled=True)  44.6 us
    unnamed x92, local copies, waits for them, and re-layouts  36 us
    dot_general x4, matrix products, rows_contract(): lax.dot_general(left, right, (((0,), (0,)), ((), ())), preferred_element_...  26 us
  transfers between devices with their start and end apart: 12, of which 6 were waited for; matrix products, arithmetic and copies ran while one was open for 61% of the time, Pallas kernels for 0%

commit v1 on v0

--- a/solution.py
+++ b/solution.py
@@ -7,6 +7,13 @@
 HEAD_DIM = 64
 EPSILON = 1e-05
 ROPE_BASE = 160000.0
+
+
+def terms_draw(m, state):
+    carry_out = jnp.concatenate([state, m], 1)
+    m_next = lax.all_gather(carry_out, "ctx", axis=0, tiled=True)
+    out_arr = jnp.split(m_next, [state.shape[1]], 1)
+    return out_arr
 
 
 def normalize(tensor):
@@ -101,8 +108,7 @@
         jnp.full((head_count, tok_rows), -1e30, f32),
         jnp.zeros((head_count, tok_rows), f32),
     )
-    key_piece = lax.all_gather(key_send, "ctx", axis=0, tiled=True)
-    value_piece = lax.all_gather(value_send, "ctx", axis=0, tiled=True)
+    key_piece, value_piece = terms_draw(value_send, key_send)
     length = key_piece.shape[0]
     step_len = math.gcd(length, 1024)
 

time: 1280 us -> 1360 us (1.062)
  waiting for transfers between devices: 373 us -> 410 us
  local copies, waits for them, and re-layouts: 82 us -> 108 us
    all_gather x1, waiting for transfers between devices: 0.01 us -> 51.1 us  [per_device(): grad_piece = lax.all_gather(grad_send, 'ctx', axis=0, tiled=True)]
    all_gather x1, waiting for transfers between devices: 128 us -> 105 us  [per_device(): lax.all_gather(in_weight, 'fsdp', axis=0, tiled=True)]
    unnamed x92 -> x94, local copies, waits for them, and re-layouts: 36 us -> 23 us
    all_gather x2 -> x3, waiting for transfers between devices: 91.9 us -> 96.2 us  [the longest x1 70.2 us: terms_draw(): m_next = lax.all_gather(carry_out, 'ctx', axis=0, tiled=True)]
  transfers between devices with their start and end apart: 12 -> 13, of which waited for: 6 -> 8; matrix products, arithmetic and copies ran while one was open for 61% -> 60% of each run, Pallas kernels for 0% -> 0%
where the time goes in v1:
time: 1360 us; the launch traced here: 1350 us
  blocking collectives  641 us (47%)
  waiting for transfers between devices  410 us (30%)
  matrix products  158 us (12%)
  local copies, waits for them, and re-layouts  108 us (8%)
  between operations  15.3 us (1%)
    unnamed x2, blocking collectives  604 us
    all_gather x1, waiting for transfers between devices, per_device(): lax.all_gather(in_weight, 'fsdp', axis=0, tiled=True)  105 us
    all_gather x1, waiting for transfers between devices, per_device(): lax.all_gather(qkv_weight, 'fsdp', axis=0, tiled=True)  80.5 us
    all_gather x1, waiting for transfers between devices, terms_draw(): m_next = lax.all_gather(carry_out, 'ctx', axis=0, tiled=True)  70.2 us
    all_gather x1, waiting for transfers between devices, per_device(): lax.all_gather(down_weight, 'fsdp', axis=0, tiled=True)  62.2 us
    all_gather x1, waiting for transfers between devices, per_device(): grad_piece = lax.all_gather(grad_send, 'ctx', axis=0, tiled=True)  51.1 us
  transfers between devices with their start and end apart: 13, of which 8 were waited for; matrix products, arithmetic and copies ran while one was open for 60% of the time, Pallas kernels for 0%

profile of v1, /device:TPU:14, one launch (start us, length us, event | category | flops | bytes accessed | tf_op | source)
XLA Modules:
  0.0 1349.5 jit_solution(487884915991531751)
XLA Ops:
  9.6 80.5 %all-gather.10.cloned.1.call-done = bf16[3072,1024]{1,0:T(8,128)(2,1)} async-done(((bf16[1536,1024]{1,0:T(8,128)(2,1)}), bf16[3072,1024]{1,0:T(8,128)(2,1)}) %all-gather.10.cloned.1.call-update) | async-done | bytes 6291472 | tf_op jit(solution)/shard_map/all_gather | solution.py:80
  90.1 5.0 fusion.85
  100.0 2.0 copy.61
  102.1 2.1 fusion.71
  109.1 70.2 %all-gather.12.cloned.1.call-done = bf16[2048,2048]{1,0:T(8,128)(2,1)} async-done(((bf16[128,2048]{1,0:T(8,128)(2,1)}), bf16[2048,2048]{1,0:T(8,128)(2,1)}) %all-gather.12.cloned.1.call-update) | async-done | bytes 8388624 | tf_op jit(solution)/shard_map/all_gather | solution.py:14
  179.3 5.9 fusion.88
  185.2 53.3 %while.48 = (s32[]{:T(128)}, f32[128,16,64]{0,2,1:T(8,128)S(1)}, f32[16,128]{1,0:T(8,128)S(1)}, f32[16,128]{1,0:T(8,128)S(1)}, bf16[2048,1024]{1,0:T(8,128)(2,1)...) while((s32[]{:T(128)}, f32[128,16,64]{0,2,1:T(8,128)S(1)}, ...), condition=%wide.region_5.0_spmd.clone, body=%wide.region_2.0_spmd.clone.sunk | while | flops 554053632 | bytes 81133776 | solution.py:135
  185.2 4.9 constant_dynamic-slice_fusion.10
  190.1 2.9 copy.92
  193.0 3.9 copy.93
  197.0 6.3 bitcast_reduce_fusion.2
  203.3 5.3 fusion.149
  210.5 4.6 constant_dynamic-slice_fusion.10
  215.1 2.9 copy.92
  218.0 3.9 copy.93
  222.0 7.7 bitcast_reduce_fusion.2
  229.7 6.0 fusion.149
  238.6 2.5 fusion.92
  241.4 105.2 %all-gather.16.cloned.1.call-done = bf16[5248,1024]{1,0:T(8,128)(2,1)} async-done(((bf16[2624,1024]{1,0:T(8,128)(2,1)}), bf16[5248,1024]{1,0:T(8,128)(2,1)}) %all-gather.16.cloned.1.call-update) | async-done | bytes 10747920 | tf_op jit(solution)/shard_map/all_gather | solution.py:82
  346.6 9.2 fusion.87
  355.8 62.2 %all-gather.18.cloned.1.call-done = bf16[1024,2624]{0,1:T(8,128)(2,1)} async-done(((bf16[512,2624]{0,1:T(8,128)(2,1)}), bf16[1024,2624]{0,1:T(8,128)(2,1)}) %all-gather.18.cloned.1.call-update) | async-done | bytes 5373968 | tf_op jit(solution)/shard_map/all_gather | solution.py:83
  418.0 5.3 fusion.48
  423.4 7.1 multiply_reduce_fusion
  432.0 2.7 fusion.75
  434.8 7.7 convolution_bitcast_fusion
  442.5 12.0 copy.78
  457.7 15.4 %all_gather.41 = f32[2048,16]{0,1:T(8,128)S(1)} all-gather(f32[128,16]{0,1:T(8,128)S(1)} %bitcast.218), channel_id=1, replica_groups=mesh['ctx'=16,'fsdp'=2] {'ctx'}, dimensions={0}, use_global_device_ids=true | all-gather | bytes 139264 | tf_op jit(solution)/shard_map/all_gather | solution.py:192
  474.2 22.1 %all_gather.43 = f32[2048,16]{0,1:T(8,128)S(1)} all-gather(f32[128,16]{0,1:T(8,128)S(1)} %multiply_reduce_fusion.1), channel_id=1, replica_groups=mesh['ctx'=16,'fsdp'=2] {'ctx'}, dimensions={0}, use_global_device_ids=true | all-gather | bytes 139264 | tf_op jit(solution)/shard_map/all_gather | solution.py:193
  496.3 26.1 %all-gather.22.cloned.1.call-done = bf16[2048,1024]{1,0:T(8,128)(2,1)} async-done(((bf16[128,1024]{1,0:T(8,128)(2,1)}), bf16[2048,1024]{1,0:T(8,128)(2,1)}) %all-gather.22.cloned.1.call-update) | async-done | bytes 4194320 | tf_op jit(solution)/shard_map/all_gather | solution.py:165
  522.4 48.5 %while.49 = (s32[]{:T(128)}, f32[128,16,64]{0,2,1:T(8,128)}, bf16[2048,1024]{1,0:T(8,128)(2,1)}, bf16[128,16,64]{0,2,1:T(8,128)(2,1)S(1)}, f32[16,128]{1,0:T(8,1...) while((s32[]{:T(128)}, f32[128,16,64]{0,2,1:T(8,128)}, ...), condition=%wide.region_12.0_spmd.clone, body=%wide.region_11.0_spmd.clone.sunk | while | flops 816185344 | bytes 41468116 | solution.py:187
  522.4 4.7 constant_dynamic-slice_fusion.11
  527.1 2.9 copy.94
  529.9 4.7 fusion.157
  534.6 3.9 copy.95
  538.6 8.0 fusion.158
  546.6 4.6 constant_dynamic-slice_fusion.11
  551.2 2.9 copy.94
  554.1 4.7 fusion.157
  558.8 3.9 copy.95
  562.7 8.2 fusion.158
  570.9 2.6 all-gather.24.cloned.1.call-done
  573.5 51.1 %all-gather.26.cloned.1.call-done = bf16[2048,1024]{1,0:T(8,128)(2,1)} async-done(((bf16[128,1024]{1,0:T(8,128)(2,1)}), bf16[2048,1024]{1,0:T(8,128)(2,1)}) %all-gather.26.cloned.1.call-update) | async-done | bytes 4194320 | tf_op jit(solution)/shard_map/all_gather | solution.py:191
  624.6 65.1 %while.50 = (s32[]{:T(128)}, f32[128,16,64]{0,2,1:T(8,128)}, f32[128,16,64]{0,2,1:T(8,128)S(1)}, bf16[2048,1024]{1,0:T(8,128)(2,1)}, bf16[128,16,64]{0,2,1:T(8,1...) while((s32[]{:T(128)}, f32[128,16,64]{0,2,1:T(8,128)}, ...), condition=%wide.region_14.0_spmd.clone, body=%wide.region_13.0_spmd.clone.sunk | while | flops 1091174400 | bytes 53412036 | solution.py:228
  624.8 4.7 constant_dynamic-slice_fusion.12
  629.5 2.9 copy.96
  632.3 4.7 fusion.166
  637.0 3.9 copy.97
  641.0 10.8 fusion.167
  651.8 5.4 fusion.168
  657.3 4.7 constant_dynamic-slice_fusion.12
  661.9 2.9 copy.96
  664.8 4.7 fusion.166
  669.5 4.0 copy.97
  673.5 10.8 fusion.167
  684.3 5.5 fusion.168
  692.5 6.4 fusion.69
  700.4 9.2 fusion.50
  709.6 552.9 %fusion = f32[168,1024]{1,0:T(8,128)} fusion(f32[5248,1024]{1,0:T(8,128)} %fusion.50), kind=kCustom, calls=%all-reduce-scatter | all-reduce-scatter fusion | flops 5505025 | bytes 22183936
  1264.5 3.8 collective-permute-start
  1268.3 4.5 fusion.49
  1272.7 8.1 collective-permute-done
  1280.9 3.1 concatenate.42
  1285.0 4.0 fusion.65
  1289.0 51.0 %all-reduce.4 = (f32[1024]{0:T(1024)S(1)}, f32[1024]{0:T(1024)S(1)}) all-reduce(f32[1024]{0:T(1024)S(1)} %get-tuple-element.613, f32[1024]{0:T(1024)S(1)} %copy-done.45), channel_id=6, replica_groups=mesh['ctx'=16,'fsdp'=2] {'ctx','fsdp'}, use_global_device_ids=true, to_apply=%region_22.0.clone | all-reduce | flops 2048 | bytes 16384
  (183 shorter events, 31.7 us)
Async XLA Ops:
  7.2 2.1 copy-start.4
  7.2 82.9 %copy-start.31 = (f32[1024]{0:T(1024)S(1)}, f32[1024]{0:T(1024)}, u32[]{:S(2)}) copy-start(f32[1024]{0:T(1024)} %param.16) | copy-start | bytes 12292
  7.2 82.9 %all-gather.10.cloned.1.call-start = ((), (), s32[]{:S(2)}) async-start(), calls=%async_computation.3 | async-start | bytes 9437184 | tf_op jit(solution)/shard_map/all_gather | solution.py:80
  7.9 171.4 %all-gather.12.cloned.1.call-start = ((), (), s32[]{:S(2)}) async-start(), calls=%async_computation.4 | async-start | bytes 8912896 | tf_op jit(solution)/shard_map/all_gather | solution.py:14
  8.2 89.5 %copy-start.27 = (f32[128,64]{0,1:T(8,128)}, f32[128,64]{0,1:T(8,128)S(1)}, u32[]{:S(2)}) copy-start(f32[128,64]{0,1:T(8,128)S(1)} %get-tuple-element.706) | copy-start | bytes 98308
  8.2 89.5 %copy-start.29 = (f32[128,64]{0,1:T(8,128)}, f32[128,64]{0,1:T(8,128)S(1)}, u32[]{:S(2)}) copy-start(f32[128,64]{0,1:T(8,128)S(1)} %get-tuple-element.705) | copy-start | bytes 98308
  9.3 80.7 %copy-start.37 = (f32[128]{0:T(128)}, f32[128]{0:T(128)S(1)}, u32[]{:S(2)}) copy-start(f32[128]{0:T(128)S(1)} %broadcast_multiply_fusion.8) | copy-start | bytes 1540
  9.6 80.5 %copy-start.39 = (f32[128]{0:T(128)}, f32[128]{0:T(128)S(1)}, u32[]{:S(2)}) copy-start(f32[128]{0:T(128)S(1)} %add_rsqrt_fusion.1) | copy-start | bytes 1540
  95.2 9.0 copy-start.10
  104.2 2.2 copy-start.18
  105.1 133.5 %all-gather.14.cloned.1.call-start = ((), (), s32[]{:S(2)}) async-start(), calls=%async_computation.5 | async-start | bytes 3145728 | tf_op jit(solution)/shard_map/all_gather | solution.py:81
  105.8 240.8 %all-gather.16.cloned.1.call-start = ((), (), s32[]{:S(2)}) async-start(), calls=%async_computation.6 | async-start | bytes 16121856 | tf_op jit(solution)/shard_map/all_gather | solution.py:82
  106.4 311.6 %all-gather.18.cloned.1.call-start = ((), (), s32[]{:S(2)}) async-start(), calls=%async_computation.7 | async-start | bytes 8060928 | tf_op jit(solution)/shard_map/all_gather | solution.py:83
  107.0 389.3 %all-gather.20.cloned.1.call-start = ((), (), s32[]{:S(2)}) async-start(), calls=%async_computation.8 | async-start | bytes 4456448 | tf_op jit(solution)/shard_map/all_gather | solution.py:164
  107.6 414.8 %all-gather.22.cloned.1.call-start = ((), (), s32[]{:S(2)}) async-start(), calls=%async_computation.9 | async-start | bytes 4456448 | tf_op jit(solution)/shard_map/all_gather | solution.py:165
  108.3 465.2 %all-gather.24.cloned.1.call-start = ((), (), s32[]{:S(2)}) async-start(), calls=%async_computation.10 | async-start | bytes 4456448 | tf_op jit(solution)/shard_map/all_gather | solution.py:190
  109.1 515.5 %all-gather.26.cloned.1.call-start = ((), (), s32[]{:S(2)}) async-start(), calls=%async_computation.11 | async-start | bytes 4456448 | tf_op jit(solution)/shard_map/all_gather | solution.py:191
  203.3 5.8 copy-start
  229.7 7.2 copy-start
  238.5 108.1 %copy-start.33 = (f32[1024]{0:T(1024)S(1)}, f32[1024]{0:T(1024)}, u32[]{:S(2)}) copy-start(f32[1024]{0:T(1024)} %param.17) | copy-start | bytes 12292
  241.1 189.4 %copy-start.1 = (f32[128,1024]{1,0:T(8,128)}, f32[128,1024]{1,0:T(8,128)S(1)}, u32[]{:S(2)}) copy-start(f32[128,1024]{1,0:T(8,128)S(1)} %get-tuple-element.708) | copy-start | bytes 1572868
  241.1 189.3 %copy-start.41 = (f32[128]{0:T(128)}, f32[128]{0:T(128)S(1)}, u32[]{:S(2)}) copy-start(f32[128]{0:T(128)S(1)} %broadcast_multiply_fusion.7) | copy-start | bytes 1540
  241.3 189.1 %copy-start.43 = (f32[128]{0:T(128)}, f32[128]{0:T(128)S(1)}, u32[]{:S(2)}) copy-start(f32[128]{0:T(128)S(1)} %add_rsqrt_fusion) | copy-start | bytes 1540
  241.4 176.7 %copy-start.22 = (bf16[1,128,1024]{2,1,0:T(8,128)(2,1)S(1)}, bf16[1,128,1024]{2,1,0:T(8,128)(2,1)}, u32[]{:S(2)}) copy-start(bf16[1,128,1024]{2,1,0:T(8,128)(2,1)} %param.15) | copy-start | bytes 786436
  423.3 7.1 copy-start.23
  423.4 7.1 copy-start.25
  423.4 7.4 copy-start.7
  430.8 4.0 copy-start.8
  432.0 910.2 %reduce-scatter.10.cloned.1.call-start = ((), (), s32[]{:S(2)}) async-start(), calls=%async_computation.13 | async-start | bytes 4325376 | tf_op jit(solution)/shard_map/reduce_scatter | solution.py:247
  434.8 907.4 %reduce-scatter.12.cloned.1.call-start = ((), (), s32[]{:S(2)}) async-start(), calls=%async_computation.14 | async-start | bytes 11354112
  454.5 0.9 copy-start.11
  454.5 1.8 copy-start.19
  454.5 887.7 %reduce-scatter.8.cloned.1.call-start = ((), (), s32[]{:S(2)}) async-start(), calls=%async_computation.12 | async-start | bytes 12976128 | tf_op jit(solution)/shard_map/reduce_scatter | solution.py:246
  457.1 0.6 copy-start.35
  522.4 102.2 %copy-start.6 = (bf16[128,16,64]{0,2,1:T(8,128)(2,1)S(1)}, bf16[128,16,64]{0,2,1:T(8,128)(2,1)}, u32[]{:S(2)}) copy-start(bf16[128,16,64]{0,2,1:T(8,128)(2,1)} %get-tuple-element.921) | copy-start | bytes 786436
  534.6 4.0 copy-start.36
  558.8 4.0 copy-start.36
  624.6 65.2 %copy-start.30 = (f32[128,64]{0,1:T(8,128)S(1)}, f32[128,64]{0,1:T(8,128)}, u32[]{:S(2)}) copy-start(f32[128,64]{0,1:T(8,128)} %copy-done.29) | copy-start | bytes 98308
  689.8 1.7 copy-start.20
  689.8 1.7 copy-start.21
  689.8 1.7 copy-start.28
  689.8 1.9 copy-start.12
  691.3 1.2 copy-start.5
  691.3 1.2 copy-start.32
  691.3 1.1 copy-start.38
  691.3 1.1 copy-start.40
  691.7 0.7 copy-start.14
  691.7 0.8 copy-start.16
  698.9 1.0 copy-start.2
  698.9 1.3 copy-start.24
  698.9 1.5 copy-start.26
  698.9 1.5 copy-start.34
  698.9 1.5 copy-start.42
  698.9 1.5 copy-start.44
  709.6 558.6 %copy-start.3 = (f32[128,5248]{1,0:T(8,128)S(1)}, f32[128,5248]{1,0:T(8,128)}, u32[]{:S(2)}) copy-start(f32[128,5248]{1,0:T(8,128)} %fusion.87) | copy-start | bytes 8060932
  1264.5 16.4 %collective-permute-start = (f32[124,1024]{1,0:T(8,128)}, f32[124,1024]{1,0:T(8,128)}, u32[]{:S(2)}, u32[]{:S(2)}) collective-permute-start(f32[124,1024]{1,0:T(8,128)} %slice.67), channel_id=1, source_target_pairs={{0,1},{1,2},{2,3},{3,4},{4,5},{5,6},{6,7},{7,8},{8,9},{9,10},{10,1... | collective-permute-start | bytes 1523720
  1272.7 12.2 copy-start.13
  1272.7 12.2 copy-start.15
  1272.7 12.2 copy-start.17
  1285.0 4.0 copy-start.45
  1285.0 56.2 %copy-start.9 = (f32[128,1024]{1,0:T(8,128)S(1)}, f32[128,1024]{1,0:T(8,128)}, u32[]{:S(2)}) copy-start(f32[128,1024]{1,0:T(8,128)} %copy-done.8) | copy-start | bytes 1572868
Sparse Core Ops, SparseCore 0:
  9.5 80.5 all-gather.9
  105.2 74.0 all-gather.11
  180.8 31.9 all-gather.13
  214.2 132.3 all-gather.15
  348.0 70.0 all-gather.17
  420.1 50.4 all-gather.19
  472.8 49.5 all-gather.21
  524.6 48.8 all-gather.23
  575.7 48.9 all-gather.25
  627.3 144.3 reduce-scatter.9
  778.2 207.4 reduce-scatter.11
  992.2 193.7 reduce-scatter.7
